TPU v7x, 256 devices: a 8x8x2 block of a 8x8x16 slice. The times are simulated.
256 devices in a mesh: grp: 2 (over z), row: 128 (over y, x, core).
Axes of the slice: x: 8, y: 8, z: 2, core: 2. Of those that a mesh axis runs over, the one named last changes fastest.
The devices are a block of a 8x8x16 slice.
Arguments:
- concentration: float32 [16, 1024, 1024], P('grp', 'row'), parts along dimension 0, may hold values from -0.95 to 1.35
- target_mass: float32 [16], P('grp'), parts along dimension 0, may hold values from 0 to 0.4
- mobility: float32 [16], P('grp'), parts along dimension 0, may hold values from 0.5 to 2
Outputs:
- updated: float32 [16, 1024, 1024], P('grp', 'row'), parts along dimension 0
- residual: float32 [16], P('grp'), parts along dimension 0
There are 2 independent parts, one for each index of `grp`. A program takes and returns all parts, laid end to end along the dimension named above; each array names one. Nothing has to cross between parts.
All inputs are finite; a program needn't handle non-finite values.
Results may differ from a plain program's by a relative error of at most 0.00005.
Values sent between devices are 32-bit elements; how exact they have to be, the bound alone decides.
A program may use at most 64 MiB of HBM per device.

v0:
```python
import math
import jax
import jax.numpy as jnp
from jax import lax
from jax.sharding import Mesh
from jax.sharding import PartitionSpec as P

ROW = ("row_0", "row_1", "row_2")
stiffness = 1.0
time_step = 0.05
stabilizer = 2.0


def by_axis(x, axes):
    for axis in axes:
        x = lax.psum(x, axis)
    return x


def make_tables(length):
    blocks = length // 128
    short_range = jnp.arange(blocks, dtype=jnp.int32)
    long_range = jnp.arange(128, dtype=jnp.int32)
    short_angle = (short_range[:, None] * short_range[None, :] % blocks).astype(jnp.float32) * (
        2.0 * math.pi / blocks
    )
    long_angle = (long_range[:, None] * long_range[None, :] % 128).astype(jnp.float32) * (
        2.0 * math.pi / 128
    )
    twist_angle = (short_range[:, None] * long_range[None, :]).astype(jnp.float32) * (
        2.0 * math.pi / length
    )
    return (
        jnp.cos(short_angle),
        jnp.sin(short_angle),
        jnp.cos(long_angle),
        jnp.sin(long_angle),
        jnp.cos(twist_angle),
        jnp.sin(twist_angle),
    )


def product(pattern, real_part, imag_part, cosine, sine, orient, real_only=False):

    def contract(operand, table):
        return jnp.einsum(pattern, operand, table, precision=lax.Precision.HIGHEST)

    if imag_part is None:
        return (contract(real_part, cosine), orient * contract(real_part, sine))
    if real_only:
        return (contract(real_part, cosine) - orient * contract(imag_part, sine), None)
    return (
        contract(real_part, cosine) - orient * contract(imag_part, sine),
        contract(imag_part, cosine) + orient * contract(real_part, sine),
    )


def rotate(real_part, imag_part, tables, orient):
    cosine, sine = (tables[4], tables[5])
    return (
        real_part * cosine - orient * imag_part * sine,
        imag_part * cosine + orient * real_part * sine,
    )


def forward_rows(real_field, tables, imag_field=None):
    planes, narrow, length = real_field.shape
    block_shape = (planes, narrow, length // 128, 128)
    shaped = real_field.reshape(block_shape)
    imag_shaped = None
    real_part, imag_part = product("pxab,ac->pxcb", shaped, imag_shaped, tables[0], tables[1], -1.0)
    real_part, imag_part = rotate(real_part, imag_part, tables, -1.0)
    real_part, imag_part = product(
        "pxcb,bd->pcdx", real_part, imag_part, tables[2], tables[3], -1.0
    )
    return (real_part.reshape(planes, length, narrow), imag_part.reshape(planes, length, narrow))


def forward_cols(pieces, tables):
    real_part, imag_part = pieces
    planes, narrow, length = real_part.shape
    shape = (planes, narrow, length // 128, 128)
    real_part, imag_part = product(
        "pqab,ac->pqcb",
        real_part.reshape(shape),
        imag_part.reshape(shape),
        tables[0],
        tables[1],
        -1.0,
    )
    real_part, imag_part = rotate(real_part, imag_part, tables, -1.0)
    real_part, imag_part = product(
        "pqcb,bd->pqcd", real_part, imag_part, tables[2], tables[3], -1.0
    )
    return (real_part.reshape(planes, narrow, length), imag_part.reshape(planes, narrow, length))


def inverse_cols(real_part, imag_part, tables):
    planes, narrow, length = real_part.shape
    shape = (planes, narrow, length // 128, 128)
    real_part, imag_part = product(
        "pqcd,db->pqcb",
        real_part.reshape(shape),
        imag_part.reshape(shape),
        tables[2],
        tables[3],
        1.0,
    )
    real_part, imag_part = rotate(real_part, imag_part, tables, 1.0)
    real_part, imag_part = product("pqcb,ca->pabq", real_part, imag_part, tables[0], tables[1], 1.0)
    return (real_part.reshape(planes, length, narrow), imag_part.reshape(planes, length, narrow))


def inverse_rows(pieces, tables):
    real_part, imag_part = pieces
    planes, narrow, length = real_part.shape
    shape = (planes, narrow, length // 128, 128)
    real_part, imag_part = product(
        "pxcd,db->pxcb",
        real_part.reshape(shape),
        imag_part.reshape(shape),
        tables[2],
        tables[3],
        1.0,
    )
    real_part, imag_part = rotate(real_part, imag_part, tables, 1.0)
    real_part, imag_part = product(
        "pxcb,ca->pxab", real_part, imag_part, tables[0], tables[1], 1.0, True
    )
    real_part = real_part.reshape(planes, narrow, length)
    return real_part


def digit_natural(positions, length):
    blocks = length // 128
    return positions // 128 + blocks * (positions % 128)


def wavenumbers(natural_index, length):
    signed = jnp.where(natural_index < length // 2, natural_index, natural_index - length)
    angular = signed.astype(jnp.float32) * (2.0 * math.pi / length)
    return (angular, jnp.where(natural_index == length // 2, jnp.float32(0.0), angular))


def local(concentration, target_mass, mobility):
    planes, rows_local, width_y = concentration.shape
    devices = lax.axis_size(ROW)
    width_x = rows_local * devices
    cols_local = width_y // devices
    cells = float(width_x * width_y)
    inverse_cells = 1.0 / cells
    residual = by_axis(jnp.sum(concentration, axis=(1, 2)), ROW) / cells - target_mass
    tables_y = make_tables(width_y)
    device = lax.axis_index(ROW)
    local_slots = jnp.arange(cols_local, dtype=jnp.int32)
    columns = device * cols_local + local_slots
    all_x = jnp.arange(width_x, dtype=jnp.int32)
    natural_x = digit_natural(all_x, width_x)
    angular_x, slope_x = wavenumbers(natural_x, width_x)
    angular_x, slope_x = (angular_x[None, :], slope_x[None, :])
    cubic_term = concentration * concentration * concentration - concentration

    def to_spectrum(pieces):
        return forward_cols(pieces, tables_y)

    angular_y, slope_y = wavenumbers(digit_natural(columns, width_y), width_y)
    stacked = jnp.concatenate([concentration, cubic_term], axis=0)
    half_real, half_imag = forward_rows(stacked, tables_y)
    spec_real, spec_imag = to_spectrum(
        (
            lax.all_to_all(half_real, ROW, split_axis=1, concat_axis=2, tiled=True),
            lax.all_to_all(half_imag, ROW, split_axis=1, concat_axis=2, tiled=True),
        )
    )
    field_real, field_imag = (spec_real[:planes], spec_imag[:planes])
    cubic_real, cubic_imag = (spec_real[planes:], spec_imag[planes:])
    angular_y, slope_y = (angular_y[:, None], slope_y[:, None])
    square = angular_x * angular_x + angular_y * angular_y
    chem_real = (cubic_real + stiffness * square * field_real) * inverse_cells
    chem_imag = (cubic_imag + stiffness * square * field_imag) * inverse_cells
    stack_real = jnp.concatenate([-slope_x * chem_imag, -slope_y * chem_imag], axis=0)
    stack_imag = jnp.concatenate([slope_x * chem_real, slope_y * chem_real], axis=0)
    back_real, back_imag = inverse_cols(stack_real, stack_imag, tables_y)
    gradient_pair = inverse_rows(
        (
            lax.all_to_all(back_real, ROW, split_axis=1, concat_axis=2, tiled=True),
            lax.all_to_all(back_imag, ROW, split_axis=1, concat_axis=2, tiled=True),
        ),
        tables_y,
    )
    grad_x = gradient_pair[:planes]
    grad_y = gradient_pair[planes:]
    weight = mobility[:, None, None] / (1.0 + concentration * concentration)
    fluxes = jnp.concatenate([weight * grad_x, weight * grad_y], axis=0)
    flux_half_real, flux_half_imag = forward_rows(fluxes, tables_y)
    flux_real, flux_imag = to_spectrum(
        (
            lax.all_to_all(flux_half_real, ROW, split_axis=1, concat_axis=2, tiled=True),
            lax.all_to_all(flux_half_imag, ROW, split_axis=1, concat_axis=2, tiled=True),
        )
    )
    flux_x_real, flux_x_imag = (flux_real[:planes], flux_imag[:planes])
    flux_y_real, flux_y_imag = (flux_real[planes:], flux_imag[planes:])
    div_real = -slope_x * flux_x_imag - slope_y * flux_y_imag
    div_imag = slope_x * flux_x_real + slope_y * flux_y_real
    factor = (
        time_step
        * inverse_cells
        / (
            1.0
            + time_step
            * mobility[:, None, None]
            * (stabilizer * square + stiffness * square * square)
        )
    )
    change_real, change_imag = inverse_cols(div_real * factor, div_imag * factor, tables_y)
    change = inverse_rows(
        (
            lax.all_to_all(change_real, ROW, split_axis=1, concat_axis=2, tiled=True),
            lax.all_to_all(change_imag, ROW, split_axis=1, concat_axis=2, tiled=True),
        ),
        tables_y,
    )
    fresh = concentration + change
    return (fresh - residual[:, None, None], residual)


def solution(mesh):
    torus = Mesh(
        mesh.devices.reshape(mesh.shape["grp"], 8, 8, 2), ("grp", "row_0", "row_1", "row_2")
    )
    in_specs = (P("grp", ROW, None), P("grp"), P("grp"))
    out_specs = (P("grp", ROW, None), P("grp"))
    return jax.shard_map(local, mesh=torus, in_specs=in_specs, out_specs=out_specs, check_vma=False)
```

profile of v0, /device:TPU:513, one launch (start us, length us, event | category | flops | bytes accessed | tf_op | source)
XLA Modules:
  0.0 410.4 jit_solution(5268577525299020385)
XLA Ops:
  13.5 28.1 %all-to-all-start.1 = ((f32[128,1,1024]{2,1,0:T(1,128)}), f32[128,1,1024]{2,1,0:T(1,128)S(1)}, u32[]{:S(2)}, u32[]{:S(2)}) async-start(f32[128,1,1024]{2,1,0:T(1,128)} %reshape.381), calls=%async_computation.1 | async-start | bytes 1048576 | tf_op jit(solution)/shard_map/all_to_all | solution.py:171
  50.8 10.3 %all-to-all-done.1 = f32[128,1,1024]{2,1,0:T(1,128)S(1)} async-done(((f32[128,1,1024]{2,1,0:T(1,128)}), f32[128,1,1024]{2,1,0:T(1,128)S(1)}, u32[]{:S(2)}, u32[]{:S(2)}) %all-to-all-start.1) | async-done | bytes 524320 | tf_op jit(solution)/shard_map/all_to_all | solution.py:171
  61.0 7.5 %all-to-all-start = ((f32[128,1,1024]{2,1,0:T(1,128)}), f32[128,1,1024]{2,1,0:T(1,128)S(1)}, u32[]{:S(2)}, u32[]{:S(2)}) async-start(f32[128,1,1024]{2,1,0:T(1,128)} %reshape.383), calls=%async_computation | async-start | bytes 1048576 | tf_op jit(solution)/shard_map/all_to_all | solution.py:172
  81.8 6.3 %all-to-all-done = f32[128,1,1024]{2,1,0:T(1,128)S(1)} async-done(((f32[128,1,1024]{2,1,0:T(1,128)}), f32[128,1,1024]{2,1,0:T(1,128)S(1)}, u32[]{:S(2)}, u32[]{:S(2)}) %all-to-all-start) | async-done | bytes 524320 | tf_op jit(solution)/shard_map/all_to_all | solution.py:172
  117.7 10.1 %all-to-all-start.2 = ((f32[128,1,1024]{2,1,0:T(1,128)}), f32[128,1,1024]{2,1,0:T(1,128)S(1)}, u32[]{:S(2)}, u32[]{:S(2)}) async-start(f32[128,1,1024]{2,1,0:T(1,128)} %reshape.387), calls=%async_computation.2 | async-start | bytes 1048576 | tf_op jit(solution)/shard_map/all_to_all | solution.py:186
  136.3 11.1 %all-to-all-done.2 = f32[128,1,1024]{2,1,0:T(1,128)S(1)} async-done(((f32[128,1,1024]{2,1,0:T(1,128)}), f32[128,1,1024]{2,1,0:T(1,128)S(1)}, u32[]{:S(2)}, u32[]{:S(2)}) %all-to-all-start.2) | async-done | bytes 524320 | tf_op jit(solution)/shard_map/all_to_all | solution.py:186
  147.4 7.5 %all-to-all-start.3 = ((f32[128,1,1024]{2,1,0:T(1,128)}), f32[128,1,1024]{2,1,0:T(1,128)S(1)}, u32[]{:S(2)}, u32[]{:S(2)}) async-start(f32[128,1,1024]{2,1,0:T(1,128)} %reshape.385), calls=%async_computation.3 | async-start | bytes 1048576 | tf_op jit(solution)/shard_map/all_to_all | solution.py:187
  162.2 6.7 %fusion.104 = f32[16,8,8,128]{3,0,2,1:T(8,128)S(1)} fusion(f32[16,8,8,128]{0,3,2,1:T(8,128)S(1)} %bitcast.292), kind=kOutput, calls=%fused_computation.167 | convolution fusion | flops 201555968 | bytes 1048576 | tf_op jit(solution)/shard_map/pxcd,db->pxcb/dot_general | solution.py:46
  168.9 6.7 %fusion.128 = f32[16,8,8,128]{3,0,2,1:T(8,128)S(1)} fusion(f32[16,8,8,128]{0,3,2,1:T(8,128)S(1)} %bitcast.293), kind=kOutput, calls=%fused_computation.191 | convolution fusion | flops 201555968 | bytes 1048576 | tf_op jit(solution)/shard_map/pxcd,db->pxcb/dot_general | solution.py:46
  183.1 6.7 %fusion.106 = f32[16,8,8,128]{3,0,2,1:T(8,128)S(1)} fusion(f32[16,8,8,128]{0,3,2,1:T(8,128)S(1)} %bitcast.294), kind=kOutput, calls=%fused_computation.169 | convolution fusion | flops 201555968 | bytes 1048576 | tf_op jit(solution)/shard_map/pxcd,db->pxcb/dot_general | solution.py:46
  189.8 6.7 %fusion.126 = f32[16,8,8,128]{3,0,2,1:T(8,128)S(1)} fusion(f32[16,8,8,128]{0,3,2,1:T(8,128)S(1)} %bitcast.295), kind=kOutput, calls=%fused_computation.189 | convolution fusion | flops 201555968 | bytes 1048576 | tf_op jit(solution)/shard_map/pxcd,db->pxcb/dot_general | solution.py:46
  210.7 17.1 %all-to-all-start.5 = ((f32[128,1,1024]{2,1,0:T(1,128)}), f32[128,1,1024]{2,1,0:T(1,128)S(1)}, u32[]{:S(2)}, u32[]{:S(2)}) async-start(f32[128,1,1024]{2,1,0:T(1,128)} %reshape.389), calls=%async_computation.5 | async-start | bytes 1048576 | tf_op jit(solution)/shard_map/all_to_all | solution.py:198
  237.0 9.9 %all-to-all-done.5 = f32[128,1,1024]{2,1,0:T(1,128)S(1)} async-done(((f32[128,1,1024]{2,1,0:T(1,128)}), f32[128,1,1024]{2,1,0:T(1,128)S(1)}, u32[]{:S(2)}, u32[]{:S(2)}) %all-to-all-start.5) | async-done | bytes 524320 | tf_op jit(solution)/shard_map/all_to_all | solution.py:198
  247.0 7.5 %all-to-all-start.4 = ((f32[128,1,1024]{2,1,0:T(1,128)}), f32[128,1,1024]{2,1,0:T(1,128)S(1)}, u32[]{:S(2)}, u32[]{:S(2)}) async-start(f32[128,1,1024]{2,1,0:T(1,128)} %reshape.391), calls=%async_computation.4 | async-start | bytes 1048576 | tf_op jit(solution)/shard_map/all_to_all | solution.py:199
  267.0 7.0 %all-to-all-done.4 = f32[128,1,1024]{2,1,0:T(1,128)S(1)} async-done(((f32[128,1,1024]{2,1,0:T(1,128)}), f32[128,1,1024]{2,1,0:T(1,128)S(1)}, u32[]{:S(2)}, u32[]{:S(2)}) %all-to-all-start.4) | async-done | bytes 524320 | tf_op jit(solution)/shard_map/all_to_all | solution.py:199
  302.4 9.3 %all-to-all-start.6 = ((f32[128,1,512]{2,1,0:T(1,128)}), f32[128,1,512]{2,1,0:T(1,128)S(1)}, u32[]{:S(2)}, u32[]{:S(2)}) async-start(f32[128,1,512]{2,1,0:T(1,128)} %reshape.395), calls=%async_computation.6 | async-start | bytes 524288 | tf_op jit(solution)/shard_map/all_to_all | solution.py:219
  315.6 4.5 %reshape.393 = f32[128,1,512]{2,1,0:T(1,128)} reshape(f32[1024,8,8]{2,1,0:T(8,128)} %bitcast.313) | data formatting | bytes 524288
  320.1 5.9 %all-to-all-done.6 = f32[128,1,512]{2,1,0:T(1,128)S(1)} async-done(((f32[128,1,512]{2,1,0:T(1,128)}), f32[128,1,512]{2,1,0:T(1,128)S(1)}, u32[]{:S(2)}, u32[]{:S(2)}) %all-to-all-start.6) | async-done | bytes 262176 | tf_op jit(solution)/shard_map/all_to_all | solution.py:219
  326.0 10.4 %all-to-all-start.7 = ((f32[128,1,512]{2,1,0:T(1,128)}), f32[128,1,512]{2,1,0:T(1,128)S(1)}, u32[]{:S(2)}, u32[]{:S(2)}) async-start(f32[128,1,512]{2,1,0:T(1,128)} %reshape.393), calls=%async_computation.7 | async-start | bytes 524288 | tf_op jit(solution)/shard_map/all_to_all | solution.py:220
  336.4 16.2 %psum.21 = f32[8]{0:T(128)S(1)} all-reduce(f32[8]{0:T(128)S(1)} %get-tuple-element.14), channel_id=1, replica_groups=mesh['grp'=2,'row_0'=8,'row_1'=8,'row_2'=2] {'row_0'}, use_global_device_ids=true, to_apply=%region_1.0 | all-reduce | flops 8 | bytes 64 | tf_op jit(solution)/shard_map/psum | solution.py:16
  352.6 12.9 %psum.22 = f32[8]{0:T(128)S(1)} all-reduce(f32[8]{0:T(128)S(1)} %psum.21), channel_id=1, replica_groups=mesh['grp'=2,'row_0'=8,'row_1'=8,'row_2'=2] {'row_1'}, use_global_device_ids=true, to_apply=%region_2.0 | all-reduce | flops 8 | bytes 64 | tf_op jit(solution)/shard_map/psum | solution.py:16
  365.5 9.7 %psum.23 = f32[8]{0:T(128)S(1)} all-reduce(f32[8]{0:T(128)S(1)} %psum.22), channel_id=1, replica_groups=mesh['grp'=2,'row_0'=8,'row_1'=8,'row_2'=2] {'row_2'}, use_global_device_ids=true, to_apply=%region_3.0 | all-reduce | flops 8 | bytes 64 | tf_op jit(solution)/shard_map/psum | solution.py:16
  380.1 6.6 %copy.147 = f32[8,8,128,8]{3,2,1,0:T(8,128)} copy(f32[8,8,128,8]{3,0,1,2:T(8,128)} %bitcast.314) | data formatting | bytes 524288 | tf_op jit(solution)/shard_map/all_to_all | solution.py:219
  395.8 6.6 %copy.150 = f32[8,8,128,8]{3,2,1,0:T(8,128)} copy(f32[8,8,128,8]{3,0,1,2:T(8,128)} %bitcast.315) | data formatting | bytes 524288 | tf_op jit(solution)/shard_map/all_to_all | solution.py:220
  (131 shorter events, 177.3 us)
Async XLA Ops:
  13.5 47.6 %all-to-all-start.1 = ((f32[128,1,1024]{2,1,0:T(1,128)}), f32[128,1,1024]{2,1,0:T(1,128)S(1)}, u32[]{:S(2)}, u32[]{:S(2)}) async-start(f32[128,1,1024]{2,1,0:T(1,128)} %reshape.381), calls=%async_computation.1 | async-start | bytes 1048576 | tf_op jit(solution)/shard_map/all_to_all | solution.py:171
  61.0 27.1 %all-to-all-start = ((f32[128,1,1024]{2,1,0:T(1,128)}), f32[128,1,1024]{2,1,0:T(1,128)S(1)}, u32[]{:S(2)}, u32[]{:S(2)}) async-start(f32[128,1,1024]{2,1,0:T(1,128)} %reshape.383), calls=%async_computation | async-start | bytes 1048576 | tf_op jit(solution)/shard_map/all_to_all | solution.py:172
  117.7 29.7 %all-to-all-start.2 = ((f32[128,1,1024]{2,1,0:T(1,128)}), f32[128,1,1024]{2,1,0:T(1,128)S(1)}, u32[]{:S(2)}, u32[]{:S(2)}) async-start(f32[128,1,1024]{2,1,0:T(1,128)} %reshape.387), calls=%async_computation.2 | async-start | bytes 1048576 | tf_op jit(solution)/shard_map/all_to_all | solution.py:186
  147.4 28.2 %all-to-all-start.3 = ((f32[128,1,1024]{2,1,0:T(1,128)}), f32[128,1,1024]{2,1,0:T(1,128)S(1)}, u32[]{:S(2)}, u32[]{:S(2)}) async-start(f32[128,1,1024]{2,1,0:T(1,128)} %reshape.385), calls=%async_computation.3 | async-start | bytes 1048576 | tf_op jit(solution)/shard_map/all_to_all | solution.py:187
  196.5 3.4 copy-start
  196.5 3.4 copy-start.1
  210.7 36.3 %all-to-all-start.5 = ((f32[128,1,1024]{2,1,0:T(1,128)}), f32[128,1,1024]{2,1,0:T(1,128)S(1)}, u32[]{:S(2)}, u32[]{:S(2)}) async-start(f32[128,1,1024]{2,1,0:T(1,128)} %reshape.389), calls=%async_computation.5 | async-start | bytes 1048576 | tf_op jit(solution)/shard_map/all_to_all | solution.py:198
  247.0 27.1 %all-to-all-start.4 = ((f32[128,1,1024]{2,1,0:T(1,128)}), f32[128,1,1024]{2,1,0:T(1,128)S(1)}, u32[]{:S(2)}, u32[]{:S(2)}) async-start(f32[128,1,1024]{2,1,0:T(1,128)} %reshape.391), calls=%async_computation.4 | async-start | bytes 1048576 | tf_op jit(solution)/shard_map/all_to_all | solution.py:199
  302.4 23.6 %all-to-all-start.6 = ((f32[128,1,512]{2,1,0:T(1,128)}), f32[128,1,512]{2,1,0:T(1,128)S(1)}, u32[]{:S(2)}, u32[]{:S(2)}) async-start(f32[128,1,512]{2,1,0:T(1,128)} %reshape.395), calls=%async_computation.6 | async-start | bytes 524288 | tf_op jit(solution)/shard_map/all_to_all | solution.py:219
  312.5 62.7 %copy-start.3 = (f32[8]{0:T(128)S(1)}, f32[8]{0:T(128)}, u32[]{:S(2)}) copy-start(f32[8]{0:T(128)} %param.4) | copy-start | bytes 100
  326.0 64.9 %all-to-all-start.7 = ((f32[128,1,512]{2,1,0:T(1,128)}), f32[128,1,512]{2,1,0:T(1,128)S(1)}, u32[]{:S(2)}, u32[]{:S(2)}) async-start(f32[128,1,512]{2,1,0:T(1,128)} %reshape.393), calls=%async_computation.7 | async-start | bytes 524288 | tf_op jit(solution)/shard_map/all_to_all | solution.py:220
  375.2 33.9 %copy-start.2 = (f32[8]{0:T(128)}, f32[8]{0:T(128)S(1)}, u32[]{:S(2)}) copy-start(f32[8]{0:T(128)S(1)} %multiply_subtract_fusion.13) | copy-start | bytes 100
where the time goes:
time: 418 us; the launch traced here: 410 us
  local copies, waits for them, and re-layouts  139 us (33%)
  starting transfers between devices  97.4 us (23%)
  matrix products  65.4 us (16%)
  waiting for transfers between devices  50.5 us (12%)
  blocking collectives  38.8 us (9%)
  other arithmetic  17.4 us (4%)
    dot_general x56, matrix products, contract(): return jnp.einsum(pattern, operand, table, precision=lax.Precision.HIGHEST)  65.4 us
    unnamed x24, local copies, waits for them, and re-layouts  58.3 us
    psum x3, blocking collectives, by_axis(): x = lax.psum(x, axis)  38.8 us
    all_to_all x1, starting transfers between devices, local(): lax.all_to_all(half_real, ROW, split_axis=1, concat_axis=2, tiled=True)  28.1 us
    all_to_all x1, starting transfers between devices, local(): lax.all_to_all(flux_half_real, ROW, split_axis=1, concat_axis=2, tiled=True)  17.1 us
    all_to_all x1, waiting for transfers between devices, local(): lax.all_to_all(back_real, ROW, split_axis=1, concat_axis=2, tiled=True)  11.1 us
    all_to_all x1, starting transfers between devices, local(): lax.all_to_all(change_imag, ROW, split_axis=1, concat_axis=2, tiled=True)  10.4 us
    all_to_all x1, waiting for transfers between devices, local(): lax.all_to_all(half_real, ROW, split_axis=1, concat_axis=2, tiled=True)  10.3 us
  transfers between devices with their start and end apart: 8, of which 6 were waited for; matrix products, arithmetic and copies ran while one was open for 24% of the time, Pallas kernels for 0%

commit v1 on v0

--- a/solution.py
+++ b/solution.py
@@ -13,7 +13,7 @@
 
 def by_axis(x, axes):
     for axis in axes:
-        x = lax.psum(x, axis)
+        x = jnp.sum(lax.all_gather(x, axis), axis=0)
     return x
 
 

time: 418 us -> 423 us (1.012)
    psum x3 -> x0, blocking collectives: 38.8 us -> none  [by_axis(): x = lax.psum(x, axis)]
    unnamed x0 -> x3, blocking collectives: none -> 38.7 us
    unnamed x24 -> x39, local copies, waits for them, and re-layouts: 58.3 us -> 60.9 us
where the time goes in v1:
time: 423 us; the launch traced here: 415 us
  local copies, waits for them, and re-layouts  142 us (34%)
  starting transfers between devices  97.5 us (23%)
  matrix products  65.4 us (15%)
  waiting for transfers between devices  50.4 us (12%)
  blocking collectives  38.7 us (9%)
  other arithmetic  17.5 us (4%)
    dot_general x56, matrix products, contract(): return jnp.einsum(pattern, operand, table, precision=lax.Precision.HIGHEST)  65.4 us
    unnamed x39, local copies, waits for them, and re-layouts  60.9 us
    unnamed x3, blocking collectives  38.7 us
    all_to_all x1, starting transfers between devices, local(): lax.all_to_all(half_real, ROW, split_axis=1, concat_axis=2, tiled=True)  28.1 us
    all_to_all x1, starting transfers between devices, local(): lax.all_to_all(flux_half_real, ROW, split_axis=1, concat_axis=2, tiled=True)  17.1 us
    all_to_all x1, waiting for transfers between devices, local(): lax.all_to_all(back_real, ROW, split_axis=1, concat_axis=2, tiled=True)  11.1 us
    all_to_all x1, starting transfers between devices, local(): lax.all_to_all(change_imag, ROW, split_axis=1, concat_axis=2, tiled=True)  10.4 us
    all_to_all x1, waiting for transfers between devices, local(): lax.all_to_all(half_real, ROW, split_axis=1, concat_axis=2, tiled=True)  10.3 us
  transfers between devices with their start and end apart: 8, of which 6 were waited for; matrix products, arithmetic and copies ran while one was open for 24% of the time, Pallas kernels for 0%

profile of v1, /device:TPU:513, one launch (start us, length us, event | category | flops | bytes accessed | tf_op | source)
XLA Modules:
  0.0 415.2 jit_solution(14711198104284512524)
XLA Ops:
  13.5 28.1 %all-to-all-start.1 = ((f32[128,1,1024]{2,1,0:T(1,128)}), f32[128,1,1024]{2,1,0:T(1,128)S(1)}, u32[]{:S(2)}, u32[]{:S(2)}) async-start(f32[128,1,1024]{2,1,0:T(1,128)} %reshape.399), calls=%async_computation.1 | async-start | bytes 1048576 | tf_op jit(solution)/shard_map/all_to_all | solution.py:171
  50.8 10.3 %all-to-all-done.1 = f32[128,1,1024]{2,1,0:T(1,128)S(1)} async-done(((f32[128,1,1024]{2,1,0:T(1,128)}), f32[128,1,1024]{2,1,0:T(1,128)S(1)}, u32[]{:S(2)}, u32[]{:S(2)}) %all-to-all-start.1) | async-done | bytes 524320 | tf_op jit(solution)/shard_map/all_to_all | solution.py:171
  61.0 7.5 %all-to-all-start = ((f32[128,1,1024]{2,1,0:T(1,128)}), f32[128,1,1024]{2,1,0:T(1,128)S(1)}, u32[]{:S(2)}, u32[]{:S(2)}) async-start(f32[128,1,1024]{2,1,0:T(1,128)} %reshape.401), calls=%async_computation | async-start | bytes 1048576 | tf_op jit(solution)/shard_map/all_to_all | solution.py:172
  81.8 6.3 %all-to-all-done = f32[128,1,1024]{2,1,0:T(1,128)S(1)} async-done(((f32[128,1,1024]{2,1,0:T(1,128)}), f32[128,1,1024]{2,1,0:T(1,128)S(1)}, u32[]{:S(2)}, u32[]{:S(2)}) %all-to-all-start) | async-done | bytes 524320 | tf_op jit(solution)/shard_map/all_to_all | solution.py:172
  117.7 10.1 %all-to-all-start.2 = ((f32[128,1,1024]{2,1,0:T(1,128)}), f32[128,1,1024]{2,1,0:T(1,128)S(1)}, u32[]{:S(2)}, u32[]{:S(2)}) async-start(f32[128,1,1024]{2,1,0:T(1,128)} %reshape.405), calls=%async_computation.2 | async-start | bytes 1048576 | tf_op jit(solution)/shard_map/all_to_all | solution.py:186
  136.3 11.1 %all-to-all-done.2 = f32[128,1,1024]{2,1,0:T(1,128)S(1)} async-done(((f32[128,1,1024]{2,1,0:T(1,128)}), f32[128,1,1024]{2,1,0:T(1,128)S(1)}, u32[]{:S(2)}, u32[]{:S(2)}) %all-to-all-start.2) | async-done | bytes 524320 | tf_op jit(solution)/shard_map/all_to_all | solution.py:186
  147.4 7.5 %all-to-all-start.3 = ((f32[128,1,1024]{2,1,0:T(1,128)}), f32[128,1,1024]{2,1,0:T(1,128)S(1)}, u32[]{:S(2)}, u32[]{:S(2)}) async-start(f32[128,1,1024]{2,1,0:T(1,128)} %reshape.403), calls=%async_computation.3 | async-start | bytes 1048576 | tf_op jit(solution)/shard_map/all_to_all | solution.py:187
  162.2 6.7 %fusion.104 = f32[16,8,8,128]{3,0,2,1:T(8,128)S(1)} fusion(f32[16,8,8,128]{0,3,2,1:T(8,128)S(1)} %bitcast.295), kind=kOutput, calls=%fused_computation.167 | convolution fusion | flops 201555968 | bytes 1048576 | tf_op jit(solution)/shard_map/pxcd,db->pxcb/dot_general | solution.py:46
  168.9 6.7 %fusion.128 = f32[16,8,8,128]{3,0,2,1:T(8,128)S(1)} fusion(f32[16,8,8,128]{0,3,2,1:T(8,128)S(1)} %bitcast.296), kind=kOutput, calls=%fused_computation.191 | convolution fusion | flops 201555968 | bytes 1048576 | tf_op jit(solution)/shard_map/pxcd,db->pxcb/dot_general | solution.py:46
  183.1 6.7 %fusion.106 = f32[16,8,8,128]{3,0,2,1:T(8,128)S(1)} fusion(f32[16,8,8,128]{0,3,2,1:T(8,128)S(1)} %bitcast.297), kind=kOutput, calls=%fused_computation.169 | convolution fusion | flops 201555968 | bytes 1048576 | tf_op jit(solution)/shard_map/pxcd,db->pxcb/dot_general | solution.py:46
  189.8 6.7 %fusion.126 = f32[16,8,8,128]{3,0,2,1:T(8,128)S(1)} fusion(f32[16,8,8,128]{0,3,2,1:T(8,128)S(1)} %bitcast.298), kind=kOutput, calls=%fused_computation.189 | convolution fusion | flops 201555968 | bytes 1048576 | tf_op jit(solution)/shard_map/pxcd,db->pxcb/dot_general | solution.py:46
  210.7 17.1 %all-to-all-start.5 = ((f32[128,1,1024]{2,1,0:T(1,128)}), f32[128,1,1024]{2,1,0:T(1,128)S(1)}, u32[]{:S(2)}, u32[]{:S(2)}) async-start(f32[128,1,1024]{2,1,0:T(1,128)} %reshape.407), calls=%async_computation.5 | async-start | bytes 1048576 | tf_op jit(solution)/shard_map/all_to_all | solution.py:198
  237.0 9.9 %all-to-all-done.5 = f32[128,1,1024]{2,1,0:T(1,128)S(1)} async-done(((f32[128,1,1024]{2,1,0:T(1,128)}), f32[128,1,1024]{2,1,0:T(1,128)S(1)}, u32[]{:S(2)}, u32[]{:S(2)}) %all-to-all-start.5) | async-done | bytes 524320 | tf_op jit(solution)/shard_map/all_to_all | solution.py:198
  247.0 7.5 %all-to-all-start.4 = ((f32[128,1,1024]{2,1,0:T(1,128)}), f32[128,1,1024]{2,1,0:T(1,128)S(1)}, u32[]{:S(2)}, u32[]{:S(2)}) async-start(f32[128,1,1024]{2,1,0:T(1,128)} %reshape.409), calls=%async_computation.4 | async-start | bytes 1048576 | tf_op jit(solution)/shard_map/all_to_all | solution.py:199
  267.1 7.0 %all-to-all-done.4 = f32[128,1,1024]{2,1,0:T(1,128)S(1)} async-done(((f32[128,1,1024]{2,1,0:T(1,128)}), f32[128,1,1024]{2,1,0:T(1,128)S(1)}, u32[]{:S(2)}, u32[]{:S(2)}) %all-to-all-start.4) | async-done | bytes 524320 | tf_op jit(solution)/shard_map/all_to_all | solution.py:199
  302.4 9.3 %all-to-all-start.6 = ((f32[128,1,512]{2,1,0:T(1,128)}), f32[128,1,512]{2,1,0:T(1,128)S(1)}, u32[]{:S(2)}, u32[]{:S(2)}) async-start(f32[128,1,512]{2,1,0:T(1,128)} %reshape.413), calls=%async_computation.6 | async-start | bytes 524288 | tf_op jit(solution)/shard_map/all_to_all | solution.py:219
  315.7 4.5 %reshape.411 = f32[128,1,512]{2,1,0:T(1,128)} reshape(f32[1024,8,8]{2,1,0:T(8,128)} %bitcast.316) | data formatting | bytes 524288
  320.2 5.9 %all-to-all-done.6 = f32[128,1,512]{2,1,0:T(1,128)S(1)} async-done(((f32[128,1,512]{2,1,0:T(1,128)}), f32[128,1,512]{2,1,0:T(1,128)S(1)}, u32[]{:S(2)}, u32[]{:S(2)}) %all-to-all-start.6) | async-done | bytes 262176 | tf_op jit(solution)/shard_map/all_to_all | solution.py:219
  326.0 10.4 %all-to-all-start.7 = ((f32[128,1,512]{2,1,0:T(1,128)}), f32[128,1,512]{2,1,0:T(1,128)S(1)}, u32[]{:S(2)}, u32[]{:S(2)}) async-start(f32[128,1,512]{2,1,0:T(1,128)} %reshape.411), calls=%async_computation.7 | async-start | bytes 524288 | tf_op jit(solution)/shard_map/all_to_all | solution.py:220
  338.0 15.7 %all-reduce = f32[64]{0:T(128)S(1)} all-reduce(f32[64]{0:T(128)S(1)} %dynamic-update-slice), channel_id=2, replica_groups=mesh['grp'=2,'row_0'=8,'row_1'=8,'row_2'=2] {'row_0'}, use_global_device_ids=true, to_apply=%add | all-reduce | flops 64 | bytes 512
  355.3 13.2 %all-reduce.1 = f32[64]{0:T(128)S(1)} all-reduce(f32[64]{0:T(128)S(1)} %dynamic-update-slice.1), channel_id=3, replica_groups=mesh['grp'=2,'row_0'=8,'row_1'=8,'row_2'=2] {'row_1'}, use_global_device_ids=true, to_apply=%add.1 | all-reduce | flops 64 | bytes 512
  370.0 9.8 %all-reduce.2 = f32[16]{0:T(128)S(1)} all-reduce(f32[16]{0:T(128)S(1)} %dynamic-update-slice.2), channel_id=4, replica_groups=mesh['grp'=2,'row_0'=8,'row_1'=8,'row_2'=2] {'row_2'}, use_global_device_ids=true, to_apply=%add.2 | all-reduce | flops 16 | bytes 128
  384.8 6.6 %copy.147 = f32[8,8,128,8]{3,2,1,0:T(8,128)} copy(f32[8,8,128,8]{3,0,1,2:T(8,128)} %bitcast.317) | data formatting | bytes 524288 | tf_op jit(solution)/shard_map/all_to_all | solution.py:219
  400.6 6.6 %copy.150 = f32[8,8,128,8]{3,2,1,0:T(8,128)} copy(f32[8,8,128,8]{3,0,1,2:T(8,128)} %bitcast.318) | data formatting | bytes 524288 | tf_op jit(solution)/shard_map/all_to_all | solution.py:220
  (152 shorter events, 180.2 us)
Async XLA Ops:
  13.5 47.6 %all-to-all-start.1 = ((f32[128,1,1024]{2,1,0:T(1,128)}), f32[128,1,1024]{2,1,0:T(1,128)S(1)}, u32[]{:S(2)}, u32[]{:S(2)}) async-start(f32[128,1,1024]{2,1,0:T(1,128)} %reshape.399), calls=%async_computation.1 | async-start | bytes 1048576 | tf_op jit(solution)/shard_map/all_to_all | solution.py:171
  61.0 27.1 %all-to-all-start = ((f32[128,1,1024]{2,1,0:T(1,128)}), f32[128,1,1024]{2,1,0:T(1,128)S(1)}, u32[]{:S(2)}, u32[]{:S(2)}) async-start(f32[128,1,1024]{2,1,0:T(1,128)} %reshape.401), calls=%async_computation | async-start | bytes 1048576 | tf_op jit(solution)/shard_map/all_to_all | solution.py:172
  117.7 29.7 %all-to-all-start.2 = ((f32[128,1,1024]{2,1,0:T(1,128)}), f32[128,1,1024]{2,1,0:T(1,128)S(1)}, u32[]{:S(2)}, u32[]{:S(2)}) async-start(f32[128,1,1024]{2,1,0:T(1,128)} %reshape.405), calls=%async_computation.2 | async-start | bytes 1048576 | tf_op jit(solution)/shard_map/all_to_all | solution.py:186
  147.4 28.2 %all-to-all-start.3 = ((f32[128,1,1024]{2,1,0:T(1,128)}), f32[128,1,1024]{2,1,0:T(1,128)S(1)}, u32[]{:S(2)}, u32[]{:S(2)}) async-start(f32[128,1,1024]{2,1,0:T(1,128)} %reshape.403), calls=%async_computation.3 | async-start | bytes 1048576 | tf_op jit(solution)/shard_map/all_to_all | solution.py:187
  196.5 3.4 copy-start
  196.5 3.4 copy-start.1
  210.7 36.3 %all-to-all-start.5 = ((f32[128,1,1024]{2,1,0:T(1,128)}), f32[128,1,1024]{2,1,0:T(1,128)S(1)}, u32[]{:S(2)}, u32[]{:S(2)}) async-start(f32[128,1,1024]{2,1,0:T(1,128)} %reshape.407), calls=%async_computation.5 | async-start | bytes 1048576 | tf_op jit(solution)/shard_map/all_to_all | solution.py:198
  247.0 27.1 %all-to-all-start.4 = ((f32[128,1,1024]{2,1,0:T(1,128)}), f32[128,1,1024]{2,1,0:T(1,128)S(1)}, u32[]{:S(2)}, u32[]{:S(2)}) async-start(f32[128,1,1024]{2,1,0:T(1,128)} %reshape.409), calls=%async_computation.4 | async-start | bytes 1048576 | tf_op jit(solution)/shard_map/all_to_all | solution.py:199
  302.4 23.6 %all-to-all-start.6 = ((f32[128,1,512]{2,1,0:T(1,128)}), f32[128,1,512]{2,1,0:T(1,128)S(1)}, u32[]{:S(2)}, u32[]{:S(2)}) async-start(f32[128,1,512]{2,1,0:T(1,128)} %reshape.413), calls=%async_computation.6 | async-start | bytes 524288 | tf_op jit(solution)/shard_map/all_to_all | solution.py:219
  312.5 23.9 %copy-start.6 = (u32[256]{0:T(256)S(1)}, u32[256]{0:T(256)}, u32[]{:S(2)}) copy-start(u32[256]{0:T(256)} %constant.147) | copy-start | bytes 3076
  312.6 41.2 %copy-start.5 = (u32[256]{0:T(256)S(1)}, u32[256]{0:T(256)}, u32[]{:S(2)}) copy-start(u32[256]{0:T(256)} %constant.152) | copy-start | bytes 3076
  312.6 55.9 %copy-start.4 = (u32[256]{0:T(256)S(1)}, u32[256]{0:T(256)}, u32[]{:S(2)}) copy-start(u32[256]{0:T(256)} %constant.157) | copy-start | bytes 3076
  312.6 67.4 %copy-start.3 = (f32[8]{0:T(128)S(1)}, f32[8]{0:T(128)}, u32[]{:S(2)}) copy-start(f32[8]{0:T(128)} %param.4) | copy-start | bytes 100
  326.0 69.7 %all-to-all-start.7 = ((f32[128,1,512]{2,1,0:T(1,128)}), f32[128,1,512]{2,1,0:T(1,128)S(1)}, u32[]{:S(2)}, u32[]{:S(2)}) async-start(f32[128,1,512]{2,1,0:T(1,128)} %reshape.411), calls=%async_computation.7 | async-start | bytes 524288 | tf_op jit(solution)/shard_map/all_to_all | solution.py:220
  380.0 33.9 %copy-start.2 = (f32[8]{0:T(128)}, f32[8]{0:T(128)S(1)}, u32[]{:S(2)}) copy-start(f32[8]{0:T(128)S(1)} %multiply_subtract_fusion.13) | copy-start | bytes 100
